TPU v7x, 128 devices: a whole 4x4x4 slice. The times are simulated.
128 devices in a mesh: row: 4 (over z_lo, core), col: 32 (over z_hi, y, x).
Axes of the slice: x: 4, y: 4, z: 4 (z_hi: 2, z_lo: 2; z = z_hi * 2 + z_lo), core: 2. Of those that a mesh axis runs over, the one named last changes fastest.
Arguments:
- left_factor: bfloat16 [4096, 8192], P('row', 'col'), may hold values from -6 to 6
- right_factor: bfloat16 [8192, 32768], P('row', 'col'), may hold values from -0.0625 to 0.0625
- matrix: float32 [4096, 32768], P('row', 'col'), may hold values from -6 to 6
- pivot_scale: float32 [8192], replicated, may hold values from 0.25 to 1.75
Outputs:
- updated: float32 [4096, 32768], P('row', 'col')
All inputs are finite; a program needn't handle non-finite values.
Results may differ from a plain program's by a relative error of at most 0.0003.
Values may be sent and summed in bfloat16 or wider, within the bound.
A program may use at most 128 MiB of HBM per device.

v0:
```python
import jax
import jax.numpy as jnp
from jax import lax
from jax.experimental import pallas as pl
from jax.experimental.pallas import tpu as pltpu
from jax.sharding import Mesh
from jax.sharding import PartitionSpec as P

MESH = pl.DeviceIdType.MESH
ROW = ("zl", "core")
COL = ("zh", "y", "x")
STAGES = 4
R = 256
HALF = R // 2
DEPTH = 256
OFFSETS = (0, -1, 1, 2)


def encode(v):
    t = v * 16.0
    t2 = t * t
    t4 = t2 * t2
    t8 = t4 * t4
    return jnp.where(t < 0.0, -t8, t8).astype(jnp.bfloat16)


def decode(c):
    y = c.astype(jnp.float32)
    r = jnp.sqrt(jnp.sqrt(jnp.sqrt(jnp.abs(y)))) * 0.0625
    return jnp.where(y < 0.0, -r, r)


def kernel(
    left, right, matrix, out, power,
    buf, bk, acc, csend, crecv, sx, sy, sz,
    send_sem, recv_sem, z_send, z_recv, c_send, c_recv, n_send, n_recv, b_send, b_recv, local_sem,
):
    x, y = lax.axis_index("x"), lax.axis_index("y")
    zl, zh, core = lax.axis_index("zl"), lax.axis_index("zh"), lax.axis_index("core")
    at = {"x": x, "y": y}
    mine = y * 4 + x

    own_b = pltpu.make_async_copy(right, bk.at[pl.ds(core * 8, 8)], local_sem.at[0])
    own_m = pltpu.make_async_copy(matrix, acc.at[pl.ds(4, 4)], local_sem.at[1])
    own_b.start()
    own_m.start()

    barrier = pltpu.get_barrier_semaphore()
    peers = [{"core": 1 - core}]
    for d in (1, 2, 3):
        peers.append({"x": lax.rem(x + d, 4)})
        peers.append({"y": lax.rem(y + d, 4)})
    peers.append({"zl": 1 - zl})
    peers.append({"zh": 1 - zh})
    peers.append({"zl": 1 - zl, "zh": 1 - zh})
    for peer in peers:
        pl.semaphore_signal(barrier, inc=1, device_id=peer, device_id_type=MESH)
    for i in range(4):
        acc[i] = jnp.zeros((R, acc.shape[2]), jnp.float32)
    pl.semaphore_wait(barrier, len(peers))

    def z_copy(sub, c, stage, zh_to, k):
        return pltpu.make_async_remote_copy(
            src_ref=left.at[sub, c], dst_ref=buf.at[stage, mine, c],
            send_sem=z_send.at[k, sub, c], recv_sem=z_recv.at[stage, c],
            device_id={"zl": zh, "zh": zh_to}, device_id_type=MESH,
        )

    inner = zh != zl

    @pl.when(inner)
    def _():
        for sub in range(2):
            for c in range(2):
                z_copy(sub, c, sub, 0, 0).start()
                z_copy(sub, c, sub, 1, 1).start()

    other_b = pltpu.make_async_remote_copy(
        src_ref=right, dst_ref=bk.at[pl.ds(core * 8, 8)],
        send_sem=b_send, recv_sem=b_recv, device_id={"core": 1 - core}, device_id_type=MESH,
    )
    other_b.start()

    def spot(c, dp, ds):
        px, py = (dp, ds) if c == 0 else (ds, dp)
        return lax.rem(y + py + 4, 4) * 4 + lax.rem(x + px + 4, 4)

    def hop(s, c, event, first, step, j, part):
        axis = "xy"[c] if first else "xy"[1 - c]
        rows = (slice(None), pl.ds(0, HALF), pl.ds(HALF, HALF))[part]
        piece = buf.at[s, j, c, rows]
        return pltpu.make_async_remote_copy(
            src_ref=piece, dst_ref=piece,
            send_sem=send_sem.at[s, c, event], recv_sem=recv_sem.at[s, c, event],
            device_id={axis: lax.rem(at[axis] + step + 4, 4)}, device_id_type=MESH,
        )

    def multiply(s, c, j):
        acc[2 * s + c] -= jnp.dot(buf[s, j, c], bk[j], preferred_element_type=jnp.float32)

    def send_column(s, c, k):
        j = spot(c, OFFSETS[k], 0)
        hop(s, c, 4 + 4 * k, False, 1, j, 0).start()
        hop(s, c, 5 + 4 * k, False, -1, j, 0).start()

    def begin(s):
        for c in range(2):
            pltpu.make_async_copy(left.at[0, 0], buf.at[s, mine, c], z_recv.at[s, c]).wait()
            hop(s, c, 0, True, 1, mine, 0).start()
            hop(s, c, 1, True, -1, mine, 0).start()
            send_column(s, c, 0)

    def first_near(s, c):
        for e, step in ((0, 1), (1, -1)):
            j = spot(c, -step, 0)
            hop(s, c, e, True, step, j, 0).wait_recv()
            hop(s, c, 2 + e, True, step, j, 1 + e).start()
            send_column(s, c, 1 + e)
            multiply(s, c, j)

    def first_far(s, c):
        j = spot(c, 2, 0)
        hop(s, c, 2, True, 1, j, 1).wait_recv()
        hop(s, c, 3, True, -1, j, 2).wait_recv()
        send_column(s, c, 3)
        multiply(s, c, j)

    def second_near(s, c, k):
        for e, step in ((0, 1), (1, -1)):
            j = spot(c, OFFSETS[k], -step)
            hop(s, c, 4 + 4 * k + e, False, step, j, 0).wait_recv()
            hop(s, c, 6 + 4 * k + e, False, step, j, 1 + e).start()
            multiply(s, c, j)

    def second_far(s, c, k):
        j = spot(c, OFFSETS[k], 2)
        hop(s, c, 6 + 4 * k, False, 1, j, 1).wait_recv()
        hop(s, c, 7 + 4 * k, False, -1, j, 2).wait_recv()
        multiply(s, c, j)

    def part_copy(i):
        return pltpu.make_async_remote_copy(
            src_ref=csend.at[i], dst_ref=crecv.at[i],
            send_sem=c_send.at[i], recv_sem=c_recv.at[i],
            device_id={"zl": 1 - zl}, device_id_type=MESH,
        )

    def fold(i):
        part_copy(i).wait_recv()
        acc[4 + i] += decode(crecv[i])

    @pl.loop(0, STAGES + 1)
    def _(s):
        fresh = s < STAGES
        old = s - 1

        @pl.when(fresh)
        def _():
            begin(s)

        @pl.when(jnp.logical_and(s == 0, jnp.logical_not(inner)))
        def _():
            for sub in range(2):
                for c in range(2):
                    pltpu.make_async_copy(
                        left.at[sub, c], buf.at[2 + sub, mine, c], z_recv.at[2 + sub, c]
                    ).start()
                    z_copy(sub, c, 2 + sub, 1 - zh, 0).start()

        @pl.when(s == 0)
        def _():
            own_b.wait()
            own_m.wait()
            other_b.wait_recv()

        @pl.when(s > 0)
        def _():
            for k in range(3):
                for c in (1, 0):
                    second_far(old, c, k)
            for c in (1, 0):
                second_near(old, c, 3)

        @pl.when(fresh)
        def _():
            for c in range(2):
                multiply(s, c, mine)
            for c in range(2):
                first_near(s, c)
            for c in (1, 0):
                second_near(s, c, 0)

        @pl.when(s > 0)
        def _():
            for c in (1, 0):
                second_far(old, c, 3)

        @pl.when(jnp.logical_and(s > 0, s < 3))
        def _():
            for c in range(2):
                csend[2 * old + c] = encode(acc[2 * old + c])
            for c in range(2):
                part_copy(2 * old + c).start()

        @pl.when(s == STAGES - 1)
        def _():
            for i in range(4):
                fold(i)

        @pl.when(fresh)
        def _():
            first_far(s, 0)
            for k in (1, 2):
                for c in range(2):
                    second_near(s, c, k)
            first_far(s, 1)

    own_out = pltpu.make_async_copy(acc.at[pl.ds(4, 4)], out, local_sem.at[0])
    own_out.start()
    for i in range(4):
        u = acc[4 + i]
        u = u * u
        t = u[:, :128]
        for j in range(1, u.shape[1] // 128):
            t = t + u[:, j * 128:(j + 1) * 128]
        sx[x, i] = jnp.sum(t.T, axis=0)

    def exchange(phase, slots, axis, me, n):
        def to(d):
            return pltpu.make_async_remote_copy(
                src_ref=slots.at[me], dst_ref=slots.at[me],
                send_sem=n_send.at[phase, d], recv_sem=n_recv.at[phase, d],
                device_id={axis: lax.rem(me + d, n)}, device_id_type=MESH,
            )

        for d in range(1, n):
            to(d).start()
        for d in range(1, n):
            came = slots.at[lax.rem(me - d + n, n)]
            pltpu.make_async_remote_copy(
                src_ref=came, dst_ref=came,
                send_sem=n_send.at[phase, d], recv_sem=n_recv.at[phase, d],
                device_id={axis: lax.rem(me + d, n)}, device_id_type=MESH,
            ).wait_recv()
        total = slots[0]
        for d in range(1, n):
            total = total + slots[d]
        return total

    sy[y] = exchange(0, sx, "x", x, 4)
    sz[zh] = exchange(1, sy, "y", y, 4)
    power[...] = exchange(2, sz, "zh", zh, 2)

    for phase, slots, axis, me, n in ((0, sx, "x", x, 4), (1, sy, "y", y, 4), (2, sz, "zh", zh, 2)):
        for d in range(1, n):
            pltpu.make_async_remote_copy(
                src_ref=slots.at[me], dst_ref=slots.at[me],
                send_sem=n_send.at[phase, d], recv_sem=n_recv.at[phase, d],
                device_id={axis: lax.rem(me + d, n)}, device_id_type=MESH,
            ).wait_send()
    for i in range(4):
        part_copy(i).wait_send()
    other_b.wait_send()

    @pl.when(inner)
    def _():
        for sub in range(2):
            for c in range(2):
                z_copy(sub, c, sub, 0, 0).wait_send()
                z_copy(sub, c, sub, 1, 1).wait_send()

    @pl.when(jnp.logical_not(inner))
    def _():
        for sub in range(2):
            for c in range(2):
                z_copy(sub, c, 2 + sub, 1 - zh, 0).wait_send()

    @pl.loop(0, STAGES)
    def _(s):
        for c in range(2):
            for e in range(20):
                far = e % 4 >= 2
                hop(s, c, e, True, 1, mine, 1 if far else 0).wait_send()
    own_out.wait()


def body(left_factor, right_factor, matrix, pivot_scale):
    share = left_factor.shape[1]
    part_scale = lax.dynamic_slice_in_dim(pivot_scale, lax.axis_index(COL) * share, share)
    scaled_left = (left_factor.astype(jnp.float32) * part_scale).astype(jnp.bfloat16)
    columns = matrix.shape[1]
    dma = pltpu.SemaphoreType.DMA
    updated, power = pl.pallas_call(
        kernel,
        out_shape=(
            jax.ShapeDtypeStruct((4, R, columns), jnp.float32),
            jax.ShapeDtypeStruct((4, R), jnp.float32),
        ),
        in_specs=[pl.BlockSpec(memory_space=pl.ANY)] * 3,
        out_specs=(pl.BlockSpec(memory_space=pl.ANY), pl.BlockSpec(memory_space=pltpu.VMEM)),
        scratch_shapes=[
            pltpu.VMEM((STAGES, 16, 2, R, DEPTH), jnp.bfloat16),
            pltpu.VMEM((16, DEPTH, columns), jnp.bfloat16),
            pltpu.VMEM((8, R, columns), jnp.float32),
            pltpu.VMEM((4, R, columns), jnp.bfloat16),
            pltpu.VMEM((4, R, columns), jnp.bfloat16),
            pltpu.VMEM((4, 4, R), jnp.float32),
            pltpu.VMEM((4, 4, R), jnp.float32),
            pltpu.VMEM((2, 4, R), jnp.float32),
            dma((STAGES, 2, 20)),
            dma((STAGES, 2, 20)),
            dma((2, 2, 2)),
            dma((STAGES, 2)),
            dma((4,)),
            dma((4,)),
            dma((3, 4)),
            dma((3, 4)),
            dma,
            dma,
            dma((2,)),
        ],
        compiler_params=pltpu.CompilerParams(collective_id=0, has_side_effects=True, vmem_limit_bytes=46 * 2**20),
        name="update",
    )(
        scaled_left.reshape(2, 2, R, DEPTH),
        right_factor.reshape(8, DEPTH, columns),
        matrix.reshape(4, R, columns),
    )
    updated = updated.reshape(matrix.shape)
    row_power = power.reshape(matrix.shape[0])
    return updated * lax.rsqrt(row_power / (columns * 32) + 1e-06)[:, None]


def solution(mesh):
    torus = Mesh(mesh.devices.reshape(2, 2, 2, 4, 4), ROW + COL)
    in_specs = (P(ROW, COL), P(ROW, COL), P(ROW, COL), P())
    return jax.shard_map(body, mesh=torus, in_specs=in_specs, out_specs=P(ROW, COL), check_vma=False)
```

profile of v0, /device:TPU:0, one launch (start us, length us, event | category | flops | bytes accessed | tf_op | source)
XLA Modules:
  0.0 121.1 jit_solution(13429998870501514531)
XLA Ops:
  0.0 0.8 dynamic_slice.3
  0.8 1.1 multiply_convert_fusion
  1.9 116.8 %update.1 = (f32[4,256,1024]{2,1,0:T(8,128)S(1)}, f32[4,256]{1,0:T(4,128)S(1)}) custom-call(bf16[2,2,256,256]{3,2,1,0:T(8,128)(2,1)S(1)} %bitcast.8, bf16[8,256,1024]{2,1,0:T(8,128)(2,1)} %bitcast.9, f32[4,256,1024]{2,1,0:T(8,128)} %bitcast.10), custom_call_target="tpu_custom_call" | custom-call | tf_op jit(solution)/shard_map/update/pallas_call | solution.py:293
  118.7 2.4 %bitcast_multiply_fusion = f32[1024,1024]{1,0:T(8,128)} fusion(f32[4,256,1024]{2,1,0:T(8,128)S(1)} %get-tuple-element.7, f32[1024]{0:T(1024)S(1)} %bitcast.11), kind=kLoop, calls=%fused_computation | loop fusion | flops 1048576 | bytes 8392704 | tf_op jit(solution)/shard_map/mul | solution.py:331
  (2 shorter events, 0.0 us)
where the time goes:
time: 121 us
  Pallas kernels  117 us (97%)
  other arithmetic  3.5 us (3%)
    pallas_call x1, Pallas kernels, body(): pl.pallas_call(kernel, out_shape=(jax.ShapeDtypeStruct((4, R, columns), j...  117 us

commit v1 on v0

--- a/solution.py
+++ b/solution.py
@@ -31,8 +31,8 @@
 
 
 def kernel(
-    left, right, matrix, out, power,
-    buf, bk, acc, csend, crecv, sx, sy, sz,
+    raw, scales, right, matrix, out, power,
+    fresh_left, scale_rows, left, buf, bk, acc, csend, crecv, sums,
     send_sem, recv_sem, z_send, z_recv, c_send, c_recv, n_send, n_recv, b_send, b_recv, local_sem,
 ):
     x, y = lax.axis_index("x"), lax.axis_index("y")
@@ -42,6 +42,10 @@
 
     own_b = pltpu.make_async_copy(right, bk.at[pl.ds(core * 8, 8)], local_sem.at[0])
     own_m = pltpu.make_async_copy(matrix, acc.at[pl.ds(4, 4)], local_sem.at[1])
+    own_left = pltpu.make_async_copy(raw, fresh_left, local_sem.at[4])
+    own_scales = pltpu.make_async_copy(scales, scale_rows, local_sem.at[5])
+    own_left.start()
+    own_scales.start()
     own_b.start()
     own_m.start()
 
@@ -57,6 +61,17 @@
         pl.semaphore_signal(barrier, inc=1, device_id=peer, device_id_type=MESH)
     for i in range(4):
         acc[i] = jnp.zeros((R, acc.shape[2]), jnp.float32)
+    own_scales.wait()
+    own_left.wait()
+    chunk = (zh * 16 + mine) * 2
+    for part in range(2):
+        columns = slice(part * 128, (part + 1) * 128)
+        scale = scale_rows[pl.ds(chunk + part, 1), :]
+        for sub in range(2):
+            for c in range(2):
+                left[sub, c, :, columns] = (
+                    fresh_left[sub, c, :, columns].astype(jnp.float32) * scale
+                ).astype(jnp.bfloat16)
     pl.semaphore_wait(barrier, len(peers))
 
     def z_copy(sub, c, stage, zh_to, k):
@@ -149,6 +164,32 @@
         part_copy(i).wait_recv()
         acc[4 + i] += decode(crecv[i])
 
+    place = (zh * 4 + y) * 4 + x
+
+    def power_copy(d):
+        dz, dy, dx = d // 16, d // 4 % 4, d % 4
+        return pltpu.make_async_remote_copy(
+            src_ref=sums.at[place], dst_ref=sums.at[place],
+            send_sem=n_send.at[d], recv_sem=n_recv.at[d],
+            device_id={
+                "zh": lax.rem(zh + dz, 2), "y": lax.rem(y + dy, 4), "x": lax.rem(x + dx, 4)
+            },
+            device_id_type=MESH,
+        )
+
+    def out_copy(half):
+        return pltpu.make_async_copy(
+            acc.at[pl.ds(4 + 2 * half, 2)], out.at[pl.ds(2 * half, 2)], local_sem.at[2 + half]
+        )
+
+    def square(i):
+        u = acc[4 + i]
+        u = u * u
+        t = u[:, :128]
+        for j in range(1, u.shape[1] // 128):
+            t = t + u[:, j * 128:(j + 1) * 128]
+        sums[place, i] = jnp.sum(t.T, axis=0)
+
     @pl.loop(0, STAGES + 1)
     def _(s):
         fresh = s < STAGES
@@ -206,6 +247,9 @@
         def _():
             for i in range(4):
                 fold(i)
+            for i in range(2):
+                square(i)
+            out_copy(0).start()
 
         @pl.when(fresh)
         def _():
@@ -215,49 +259,20 @@
                     second_near(s, c, k)
             first_far(s, 1)
 
-    own_out = pltpu.make_async_copy(acc.at[pl.ds(4, 4)], out, local_sem.at[0])
-    own_out.start()
-    for i in range(4):
-        u = acc[4 + i]
-        u = u * u
-        t = u[:, :128]
-        for j in range(1, u.shape[1] // 128):
-            t = t + u[:, j * 128:(j + 1) * 128]
-        sx[x, i] = jnp.sum(t.T, axis=0)
-
-    def exchange(phase, slots, axis, me, n):
-        def to(d):
-            return pltpu.make_async_remote_copy(
-                src_ref=slots.at[me], dst_ref=slots.at[me],
-                send_sem=n_send.at[phase, d], recv_sem=n_recv.at[phase, d],
-                device_id={axis: lax.rem(me + d, n)}, device_id_type=MESH,
-            )
-
-        for d in range(1, n):
-            to(d).start()
-        for d in range(1, n):
-            came = slots.at[lax.rem(me - d + n, n)]
-            pltpu.make_async_remote_copy(
-                src_ref=came, dst_ref=came,
-                send_sem=n_send.at[phase, d], recv_sem=n_recv.at[phase, d],
-                device_id={axis: lax.rem(me + d, n)}, device_id_type=MESH,
-            ).wait_recv()
-        total = slots[0]
-        for d in range(1, n):
-            total = total + slots[d]
-        return total
-
-    sy[y] = exchange(0, sx, "x", x, 4)
-    sz[zh] = exchange(1, sy, "y", y, 4)
-    power[...] = exchange(2, sz, "zh", zh, 2)
-
-    for phase, slots, axis, me, n in ((0, sx, "x", x, 4), (1, sy, "y", y, 4), (2, sz, "zh", zh, 2)):
-        for d in range(1, n):
-            pltpu.make_async_remote_copy(
-                src_ref=slots.at[me], dst_ref=slots.at[me],
-                send_sem=n_send.at[phase, d], recv_sem=n_recv.at[phase, d],
-                device_id={axis: lax.rem(me + d, n)}, device_id_type=MESH,
-            ).wait_send()
+    for i in (2, 3):
+        square(i)
+    out_copy(1).start()
+    for d in range(31, 0, -1):
+        power_copy(d).start()
+    for d in range(1, 32):
+        power_copy(d).wait_recv()
+    total = sums[0]
+    for d in range(1, 32):
+        total = total + sums[d]
+    power[...] = total
+
+    for d in range(1, 32):
+        power_copy(d).wait_send()
     for i in range(4):
         part_copy(i).wait_send()
     other_b.wait_send()
@@ -281,13 +296,11 @@
             for e in range(20):
                 far = e % 4 >= 2
                 hop(s, c, e, True, 1, mine, 1 if far else 0).wait_send()
-    own_out.wait()
+    out_copy(0).wait()
+    out_copy(1).wait()
 
 
 def body(left_factor, right_factor, matrix, pivot_scale):
-    share = left_factor.shape[1]
-    part_scale = lax.dynamic_slice_in_dim(pivot_scale, lax.axis_index(COL) * share, share)
-    scaled_left = (left_factor.astype(jnp.float32) * part_scale).astype(jnp.bfloat16)
     columns = matrix.shape[1]
     dma = pltpu.SemaphoreType.DMA
     updated, power = pl.pallas_call(
@@ -296,33 +309,35 @@
             jax.ShapeDtypeStruct((4, R, columns), jnp.float32),
             jax.ShapeDtypeStruct((4, R), jnp.float32),
         ),
-        in_specs=[pl.BlockSpec(memory_space=pl.ANY)] * 3,
+        in_specs=[pl.BlockSpec(memory_space=pl.ANY)] * 4,
         out_specs=(pl.BlockSpec(memory_space=pl.ANY), pl.BlockSpec(memory_space=pltpu.VMEM)),
         scratch_shapes=[
+            pltpu.VMEM((2, 2, R, DEPTH), jnp.bfloat16),
+            pltpu.VMEM((64, 128), jnp.float32),
+            pltpu.VMEM((2, 2, R, DEPTH), jnp.bfloat16),
             pltpu.VMEM((STAGES, 16, 2, R, DEPTH), jnp.bfloat16),
             pltpu.VMEM((16, DEPTH, columns), jnp.bfloat16),
             pltpu.VMEM((8, R, columns), jnp.float32),
             pltpu.VMEM((4, R, columns), jnp.bfloat16),
             pltpu.VMEM((4, R, columns), jnp.bfloat16),
-            pltpu.VMEM((4, 4, R), jnp.float32),
-            pltpu.VMEM((4, 4, R), jnp.float32),
-            pltpu.VMEM((2, 4, R), jnp.float32),
+            pltpu.VMEM((32, 4, R), jnp.float32),
             dma((STAGES, 2, 20)),
             dma((STAGES, 2, 20)),
             dma((2, 2, 2)),
             dma((STAGES, 2)),
             dma((4,)),
             dma((4,)),
-            dma((3, 4)),
-            dma((3, 4)),
+            dma((32,)),
+            dma((32,)),
             dma,
             dma,
-            dma((2,)),
+            dma((6,)),
         ],
         compiler_params=pltpu.CompilerParams(collective_id=0, has_side_effects=True, vmem_limit_bytes=46 * 2**20),
         name="update",
     )(
-        scaled_left.reshape(2, 2, R, DEPTH),
+        pltpu.with_memory_space_constraint(left_factor.reshape(2, 2, R, DEPTH), pltpu.HBM),
+        pltpu.with_memory_space_constraint(pivot_scale.reshape(64, 128), pltpu.HBM),
         right_factor.reshape(8, DEPTH, columns),
         matrix.reshape(4, R, columns),
     )

time: 121 us -> 116 us (0.959)
  Pallas kernels: 117 us -> 114 us
    pallas_call x1, Pallas kernels: 117 us -> 114 us  [body(): pl.pallas_call(kernel, out_shape=(jax.ShapeDtypeStruct((4, R, columns), j...]
where the time goes in v1:
time: 116 us
  Pallas kernels  114 us (98%)
  other arithmetic  2.36 us (2%)
    pallas_call x1, Pallas kernels, body(): pl.pallas_call(kernel, out_shape=(jax.ShapeDtypeStruct((4, R, columns), j...  114 us
    mul x1, other arithmetic, body(): return updated * lax.rsqrt(row_power / (columns * 32) + 1e-06)[:, None]  2.35 us

profile of v1, /device:TPU:0, one launch (start us, length us, event | category | flops | bytes accessed | tf_op | source)
XLA Modules:
  0.0 116.0 jit_solution(1980226187159424975)
XLA Ops:
  0.0 113.6 %update.1 = (f32[4,256,1024]{2,1,0:T(8,128)S(1)}, f32[4,256]{1,0:T(4,128)S(1)}) custom-call(bf16[2,2,256,256]{3,2,1,0:T(8,128)(2,1)} %bitcast.11, f32[64,128]{1,0:T(8,128)} %bitcast.12, bf16[8,256,1024]{2,1,0:T(8,128)(2,1)} %bitcast.9, f32[4,256,1024]{2,1,0:T(8,128)} %bitcast.10), custom_call_target="tpu_custom_call" | custom-call | tf_op jit(solution)/shard_map/update/pallas_call | solution.py:306
  113.7 2.4 %bitcast_multiply_fusion = f32[1024,1024]{1,0:T(8,128)} fusion(f32[4,256,1024]{2,1,0:T(8,128)S(1)} %get-tuple-element.7, f32[1024]{0:T(1024)S(1)} %bitcast.13), kind=kLoop, calls=%fused_computation | loop fusion | flops 1048576 | bytes 8392704 | tf_op jit(solution)/shard_map/mul | solution.py:346
  (2 shorter events, 0.0 us)

commit v2 on v1

--- a/solution.py
+++ b/solution.py
@@ -13,6 +13,7 @@
 R = 256
 HALF = R // 2
 DEPTH = 256
+HALVES = (pl.ds(0, HALF), pl.ds(HALF, HALF))
 OFFSETS = (0, -1, 1, 2)
 
 
@@ -26,7 +27,7 @@
 
 def decode(c):
     y = c.astype(jnp.float32)
-    r = jnp.sqrt(jnp.sqrt(jnp.sqrt(jnp.abs(y)))) * 0.0625
+    r = jnp.exp2(jnp.log2(jnp.abs(y)) * 0.125 - 4.0)
     return jnp.where(y < 0.0, -r, r)
 
 
@@ -51,12 +52,11 @@
 
     barrier = pltpu.get_barrier_semaphore()
     peers = [{"core": 1 - core}]
-    for d in (1, 2, 3):
+    for d in (1, 3):
         peers.append({"x": lax.rem(x + d, 4)})
         peers.append({"y": lax.rem(y + d, 4)})
-    peers.append({"zl": 1 - zl})
-    peers.append({"zh": 1 - zh})
-    peers.append({"zl": 1 - zl, "zh": 1 - zh})
+        z = lax.rem(2 * zh + zl + d, 4)
+        peers.append({"zh": z // 2, "zl": lax.rem(z, 2)})
     for peer in peers:
         pl.semaphore_signal(barrier, inc=1, device_id=peer, device_id_type=MESH)
     for i in range(4):
@@ -74,10 +74,10 @@
                 ).astype(jnp.bfloat16)
     pl.semaphore_wait(barrier, len(peers))
 
-    def z_copy(sub, c, stage, zh_to, k):
+    def z_copy(sub, c, p, stage, zh_to, k):
         return pltpu.make_async_remote_copy(
-            src_ref=left.at[sub, c], dst_ref=buf.at[stage, mine, c],
-            send_sem=z_send.at[k, sub, c], recv_sem=z_recv.at[stage, c],
+            src_ref=left.at[sub, c, HALVES[p]], dst_ref=buf.at[stage, mine, c, HALVES[p]],
+            send_sem=z_send.at[k, sub, c, p], recv_sem=z_recv.at[stage, c, p],
             device_id={"zl": zh, "zh": zh_to}, device_id_type=MESH,
         )
 
@@ -87,8 +87,9 @@
     def _():
         for sub in range(2):
             for c in range(2):
-                z_copy(sub, c, sub, 0, 0).start()
-                z_copy(sub, c, sub, 1, 1).start()
+                for p in range(2):
+                    z_copy(sub, c, p, sub, 0, 0).start()
+                    z_copy(sub, c, p, sub, 1, 1).start()
 
     other_b = pltpu.make_async_remote_copy(
         src_ref=right, dst_ref=bk.at[pl.ds(core * 8, 8)],
@@ -120,10 +121,14 @@
 
     def begin(s):
         for c in range(2):
-            pltpu.make_async_copy(left.at[0, 0], buf.at[s, mine, c], z_recv.at[s, c]).wait()
-            hop(s, c, 0, True, 1, mine, 0).start()
-            hop(s, c, 1, True, -1, mine, 0).start()
-            send_column(s, c, 0)
+            for p in range(2):
+                pltpu.make_async_copy(
+                    left.at[0, 0, HALVES[0]], buf.at[s, mine, c, HALVES[p]], z_recv.at[s, c, p]
+                ).wait()
+                hop(s, c, 0, True, 1, mine, 1 + p).start()
+                hop(s, c, 1, True, -1, mine, 1 + p).start()
+                hop(s, c, 4, False, 1, mine, 1 + p).start()
+                hop(s, c, 5, False, -1, mine, 1 + p).start()
 
     def first_near(s, c):
         for e, step in ((0, 1), (1, -1)):
@@ -190,74 +195,91 @@
             t = t + u[:, j * 128:(j + 1) * 128]
         sums[place, i] = jnp.sum(t.T, axis=0)
 
-    @pl.loop(0, STAGES + 1)
-    def _(s):
-        fresh = s < STAGES
-        old = s - 1
-
-        @pl.when(fresh)
-        def _():
-            begin(s)
-
-        @pl.when(jnp.logical_and(s == 0, jnp.logical_not(inner)))
+    @pl.loop(0, STAGES + 2)
+    def _(r):
+        new, mid, old = r, r - 1, r - 2
+        starts = r < STAGES
+        passes = jnp.logical_and(r >= 1, r < STAGES + 1)
+        ends = r >= 2
+
+        @pl.when(starts)
+        def _():
+            begin(new)
+
+        @pl.when(jnp.logical_and(r == 1, jnp.logical_not(inner)))
         def _():
             for sub in range(2):
                 for c in range(2):
-                    pltpu.make_async_copy(
-                        left.at[sub, c], buf.at[2 + sub, mine, c], z_recv.at[2 + sub, c]
-                    ).start()
-                    z_copy(sub, c, 2 + sub, 1 - zh, 0).start()
-
-        @pl.when(s == 0)
+                    for p in range(2):
+                        pltpu.make_async_copy(
+                            left.at[sub, c, HALVES[p]], buf.at[2 + sub, mine, c, HALVES[p]],
+                            z_recv.at[2 + sub, c, p],
+                        ).start()
+            for c in range(2):
+                for p in range(2):
+                    z_copy(0, c, p, 2, 1 - zh, 0).start()
+
+        @pl.when(jnp.logical_and(r == 2, jnp.logical_not(inner)))
+        def _():
+            for c in range(2):
+                for p in range(2):
+                    z_copy(1, c, p, 3, 1 - zh, 0).start()
+
+        @pl.when(r == 0)
         def _():
             own_b.wait()
             own_m.wait()
             other_b.wait_recv()
 
-        @pl.when(s > 0)
-        def _():
-            for k in range(3):
-                for c in (1, 0):
+        @pl.when(passes)
+        def _():
+            first_far(mid, 0)
+            for c in range(2):
+                second_near(mid, c, 0)
+            first_far(mid, 1)
+
+        @pl.when(ends)
+        def _():
+            for k in (2, 1, 0):
+                for c in range(2):
                     second_far(old, c, k)
-            for c in (1, 0):
-                second_near(old, c, 3)
-
-        @pl.when(fresh)
-        def _():
-            for c in range(2):
-                multiply(s, c, mine)
-            for c in range(2):
-                first_near(s, c)
-            for c in (1, 0):
-                second_near(s, c, 0)
-
-        @pl.when(s > 0)
-        def _():
-            for c in (1, 0):
+
+        @pl.when(r == STAGES + 1)
+        def _():
+            fold(2)
+            fold(3)
+
+        @pl.when(ends)
+        def _():
+            for c in range(2):
                 second_far(old, c, 3)
 
-        @pl.when(jnp.logical_and(s > 0, s < 3))
+        @pl.when(jnp.logical_and(ends, r < 4))
         def _():
             for c in range(2):
                 csend[2 * old + c] = encode(acc[2 * old + c])
             for c in range(2):
                 part_copy(2 * old + c).start()
 
-        @pl.when(s == STAGES - 1)
-        def _():
-            for i in range(4):
+        @pl.when(starts)
+        def _():
+            for c in range(2):
+                multiply(new, c, mine)
+            for c in range(2):
+                first_near(new, c)
+
+        @pl.when(passes)
+        def _():
+            for k in (2, 1, 3):
+                for c in range(2):
+                    second_near(mid, c, k)
+
+        @pl.when(r == STAGES)
+        def _():
+            for i in range(2):
                 fold(i)
-            for i in range(2):
                 square(i)
             out_copy(0).start()
-
-        @pl.when(fresh)
-        def _():
-            first_far(s, 0)
-            for k in (1, 2):
-                for c in range(2):
-                    second_near(s, c, k)
-            first_far(s, 1)
 
     for i in (2, 3):
         square(i)
@@ -281,14 +303,16 @@
     def _():
         for sub in range(2):
             for c in range(2):
-                z_copy(sub, c, sub, 0, 0).wait_send()
-                z_copy(sub, c, sub, 1, 1).wait_send()
+                for p in range(2):
+                    z_copy(sub, c, p, sub, 0, 0).wait_send()
+                    z_copy(sub, c, p, sub, 1, 1).wait_send()
 
     @pl.when(jnp.logical_not(inner))
     def _():
         for sub in range(2):
             for c in range(2):
-                z_copy(sub, c, 2 + sub, 1 - zh, 0).wait_send()
+                for p in range(2):
+                    z_copy(sub, c, p, 2 + sub, 1 - zh, 0).wait_send()
 
     @pl.loop(0, STAGES)
     def _(s):
@@ -323,8 +347,8 @@
             pltpu.VMEM((32, 4, R), jnp.float32),
             dma((STAGES, 2, 20)),
             dma((STAGES, 2, 20)),
-            dma((2, 2, 2)),
-            dma((STAGES, 2)),
+            dma((2, 2, 2, 2)),
+            dma((STAGES, 2, 2)),
             dma((4,)),
             dma((4,)),
             dma((32,)),

time: 116 us -> 111 us (0.957)
  Pallas kernels: 114 us -> 109 us
    pallas_call x1, Pallas kernels: 114 us -> 109 us  [body(): pl.pallas_call(kernel, out_shape=(jax.ShapeDtypeStruct((4, R, columns), j...]
where the time goes in v2:
time: 111 us
  Pallas kernels  109 us (98%)
  other arithmetic  2.36 us (2%)
    pallas_call x1, Pallas kernels, body(): pl.pallas_call(kernel, out_shape=(jax.ShapeDtypeStruct((4, R, columns), j...  109 us
    mul x1, other arithmetic, body(): return updated * lax.rsqrt(row_power / (columns * 32) + 1e-06)[:, None]  2.35 us

profile of v2, /device:TPU:0, one launch (start us, length us, event | category | flops | bytes accessed | tf_op | source)
XLA Modules:
  0.0 111.1 jit_solution(13136433781993879089)
XLA Ops:
  0.0 108.7 %update.1 = (f32[4,256,1024]{2,1,0:T(8,128)S(1)}, f32[4,256]{1,0:T(4,128)S(1)}) custom-call(bf16[2,2,256,256]{3,2,1,0:T(8,128)(2,1)} %bitcast.11, f32[64,128]{1,0:T(8,128)} %bitcast.12, bf16[8,256,1024]{2,1,0:T(8,128)(2,1)} %bitcast.9, f32[4,256,1024]{2,1,0:T(8,128)} %bitcast.10), custom_call_target="tpu_custom_call" | custom-call | tf_op jit(solution)/shard_map/update/pallas_call | solution.py:330
  108.7 2.4 %bitcast_multiply_fusion = f32[1024,1024]{1,0:T(8,128)} fusion(f32[4,256,1024]{2,1,0:T(8,128)S(1)} %get-tuple-element.7, f32[1024]{0:T(1024)S(1)} %bitcast.13), kind=kLoop, calls=%fused_computation | loop fusion | flops 1048576 | bytes 8392704 | tf_op jit(solution)/shard_map/mul | solution.py:370
  (2 shorter events, 0.0 us)

commit v3 on v2

--- a/solution.py
+++ b/solution.py
@@ -234,15 +234,18 @@
         @pl.when(passes)
         def _():
             first_far(mid, 0)
-            for c in range(2):
-                second_near(mid, c, 0)
+            second_near(mid, 0, 0)
+            second_near(mid, 1, 0)
             first_far(mid, 1)
 
         @pl.when(ends)
         def _():
-            for k in (2, 1, 0):
-                for c in range(2):
-                    second_far(old, c, k)
+            second_far(old, 1, 2)
+            second_far(old, 0, 2)
+            second_far(old, 0, 1)
+            second_far(old, 1, 1)
+            second_far(old, 0, 0)
+            second_far(old, 1, 0)
 
         @pl.when(r == STAGES + 1)
         def _():
@@ -251,8 +254,8 @@
 
         @pl.when(ends)
         def _():
-            for c in range(2):
-                second_far(old, c, 3)
+            second_far(old, 0, 3)
+            second_far(old, 1, 3)
 
         @pl.when(jnp.logical_and(ends, r < 4))
         def _():
@@ -263,16 +266,19 @@
 
         @pl.when(starts)
         def _():
-            for c in range(2):
-                multiply(new, c, mine)
-            for c in range(2):
-                first_near(new, c)
+            multiply(new, 0, mine)
+            first_near(new, 0)
+            multiply(new, 1, mine)
+            first_near(new, 1)
 
         @pl.when(passes)
         def _():
-            for k in (2, 1, 3):
-                for c in range(2):
-                    second_near(mid, c, k)
+            second_near(mid, 0, 2)
+            second_near(mid, 1, 2)
+            second_near(mid, 0, 1)
+            second_near(mid, 1, 1)
+            second_near(mid, 0, 3)
+            second_near(mid, 1, 3)
 
         @pl.when(r == STAGES)
         def _():
@@ -284,7 +290,7 @@
     for i in (2, 3):
         square(i)
     out_copy(1).start()
-    for d in range(31, 0, -1):
+    for d in sorted(range(1, 32), key=lambda d: -sum((d // 16 * 2, min(d // 4 % 4, 4 - d // 4 % 4), min(d % 4, 4 - d % 4)))):
         power_copy(d).start()
     for d in range(1, 32):
         power_copy(d).wait_recv()

time: 111 us -> 111 us (level)
  no operation moved by 1% of the time
where the time goes in v3:
time: 111 us
  Pallas kernels  109 us (98%)
  other arithmetic  2.36 us (2%)
    pallas_call x1, Pallas kernels, body(): pl.pallas_call(kernel, out_shape=(jax.ShapeDtypeStruct((4, R, columns), j...  109 us
    mul x1, other arithmetic, body(): return updated * lax.rsqrt(row_power / (columns * 32) + 1e-06)[:, None]  2.35 us

profile of v3, /device:TPU:0, one launch (start us, length us, event | category | flops | bytes accessed | tf_op | source)
XLA Modules:
  0.0 111.0 jit_solution(4065138879853128838)
XLA Ops:
  0.0 108.6 %update.1 = (f32[4,256,1024]{2,1,0:T(8,128)S(1)}, f32[4,256]{1,0:T(4,128)S(1)}) custom-call(bf16[2,2,256,256]{3,2,1,0:T(8,128)(2,1)} %bitcast.11, f32[64,128]{1,0:T(8,128)} %bitcast.12, bf16[8,256,1024]{2,1,0:T(8,128)(2,1)} %bitcast.9, f32[4,256,1024]{2,1,0:T(8,128)} %bitcast.10), custom_call_target="tpu_custom_call" | custom-call | tf_op jit(solution)/shard_map/update/pallas_call | solution.py:336
  108.6 2.4 %bitcast_multiply_fusion = f32[1024,1024]{1,0:T(8,128)} fusion(f32[4,256,1024]{2,1,0:T(8,128)S(1)} %get-tuple-element.7, f32[1024]{0:T(1024)S(1)} %bitcast.13), kind=kLoop, calls=%fused_computation | loop fusion | flops 1048576 | bytes 8392704 | tf_op jit(solution)/shard_map/mul | solution.py:376
  (2 shorter events, 0.0 us)

commit v4 on v3

--- a/solution.py
+++ b/solution.py
@@ -247,11 +247,6 @@
             second_far(old, 0, 0)
             second_far(old, 1, 0)
 
-        @pl.when(r == STAGES + 1)
-        def _():
-            fold(2)
-            fold(3)
-
         @pl.when(ends)
         def _():
             second_far(old, 0, 3)
@@ -286,6 +281,8 @@
                 fold(i)
                 square(i)
             out_copy(0).start()
+            fold(2)
+            fold(3)
 
     for i in (2, 3):
         square(i)

time: 111 us -> 111 us (level)
  no operation moved by 1% of the time
where the time goes in v4:
time: 111 us
  Pallas kernels  109 us (98%)
  other arithmetic  2.36 us (2%)
    pallas_call x1, Pallas kernels, body(): pl.pallas_call(kernel, out_shape=(jax.ShapeDtypeStruct((4, R, columns), j...  109 us
    mul x1, other arithmetic, body(): return updated * lax.rsqrt(row_power / (columns * 32) + 1e-06)[:, None]  2.35 us

profile of v4, /device:TPU:0, one launch (start us, length us, event | category | flops | bytes accessed | tf_op | source)
XLA Modules:
  0.0 111.0 jit_solution(9364275586474868645)
XLA Ops:
  0.0 108.6 %update.1 = (f32[4,256,1024]{2,1,0:T(8,128)S(1)}, f32[4,256]{1,0:T(4,128)S(1)}) custom-call(bf16[2,2,256,256]{3,2,1,0:T(8,128)(2,1)} %bitcast.11, f32[64,128]{1,0:T(8,128)} %bitcast.12, bf16[8,256,1024]{2,1,0:T(8,128)(2,1)} %bitcast.9, f32[4,256,1024]{2,1,0:T(8,128)} %bitcast.10), custom_call_target="tpu_custom_call" | custom-call | tf_op jit(solution)/shard_map/update/pallas_call | solution.py:333
  108.6 2.4 %bitcast_multiply_fusion = f32[1024,1024]{1,0:T(8,128)} fusion(f32[4,256,1024]{2,1,0:T(8,128)S(1)} %get-tuple-element.7, f32[1024]{0:T(1024)S(1)} %bitcast.13), kind=kLoop, calls=%fused_computation | loop fusion | flops 1048576 | bytes 8392704 | tf_op jit(solution)/shard_map/mul | solution.py:373
  (2 shorter events, 0.0 us)

commit v5 on v3

--- a/solution.py
+++ b/solution.py
@@ -136,7 +136,8 @@
             hop(s, c, e, True, step, j, 0).wait_recv()
             hop(s, c, 2 + e, True, step, j, 1 + e).start()
             send_column(s, c, 1 + e)
-            multiply(s, c, j)
+        for step in (1, -1):
+            multiply(s, c, spot(c, -step, 0))
 
     def first_far(s, c):
         j = spot(c, 2, 0)
@@ -150,7 +151,8 @@
             j = spot(c, OFFSETS[k], -step)
             hop(s, c, 4 + 4 * k + e, False, step, j, 0).wait_recv()
             hop(s, c, 6 + 4 * k + e, False, step, j, 1 + e).start()
-            multiply(s, c, j)
+        for step in (1, -1):
+            multiply(s, c, spot(c, OFFSETS[k], -step))
 
     def second_far(s, c, k):
         j = spot(c, OFFSETS[k], 2)

time: 111 us -> 111 us (level)
  no operation moved by 1% of the time
where the time goes in v5:
time: 111 us
  Pallas kernels  109 us (98%)
  other arithmetic  2.36 us (2%)
    pallas_call x1, Pallas kernels, body(): pl.pallas_call(kernel, out_shape=(jax.ShapeDtypeStruct((4, R, columns), j...  109 us
    mul x1, other arithmetic, body(): return updated * lax.rsqrt(row_power / (columns * 32) + 1e-06)[:, None]  2.35 us

profile of v5, /device:TPU:0, one launch (start us, length us, event | category | flops | bytes accessed | tf_op | source)
XLA Modules:
  0.0 111.0 jit_solution(13017764683649296628)
XLA Ops:
  0.0 108.6 %update.1 = (f32[4,256,1024]{2,1,0:T(8,128)S(1)}, f32[4,256]{1,0:T(4,128)S(1)}) custom-call(bf16[2,2,256,256]{3,2,1,0:T(8,128)(2,1)} %bitcast.11, f32[64,128]{1,0:T(8,128)} %bitcast.12, bf16[8,256,1024]{2,1,0:T(8,128)(2,1)} %bitcast.9, f32[4,256,1024]{2,1,0:T(8,128)} %bitcast.10), custom_call_target="tpu_custom_call" | custom-call | tf_op jit(solution)/shard_map/update/pallas_call | solution.py:338
  108.6 2.4 %bitcast_multiply_fusion = f32[1024,1024]{1,0:T(8,128)} fusion(f32[4,256,1024]{2,1,0:T(8,128)S(1)} %get-tuple-element.7, f32[1024]{0:T(1024)S(1)} %bitcast.13), kind=kLoop, calls=%fused_computation | loop fusion | flops 1048576 | bytes 8392704 | tf_op jit(solution)/shard_map/mul | solution.py:378
  (2 shorter events, 0.0 us)
